TPU v7x, 32 devices: a whole 2x2x4 slice. The times are simulated.
32 devices in a mesh: depth: 4 (over y, x), area: 8 (over z, core).
Axes of the slice: x: 2, y: 2, z: 4, core: 2. Of those that a mesh axis runs over, the one named last changes fastest.
Arguments:
- states: float32 [8, 64, 128, 768], P(None, 'depth', 'area'), may hold values from 0 to 1
- tissue: int32 [16, 32, 192], P('depth', 'area'), may hold values 0 or 1
- fiber: int32 [16, 32, 192], P('depth', 'area'), may hold values from 0 to 7
Outputs:
- final_states: float32 [8, 64, 128, 768], P(None, 'depth', 'area')
- images: float32 [2, 2, 4, 128, 768], P(None, None, None, 'area', 'depth')
All inputs are finite; a program needn't handle non-finite values. No bound on the sum of `tissue` on one device may be relied on, other than what follows from the above.
Results may differ from a plain program's by a relative error of at most 0.0002.
Values sent between devices are 32-bit elements; how exact they have to be, the bound alone decides.
A program may use at most 128 MiB of HBM per device.

v0:
```python
import math

import jax
import jax.numpy as jnp
from jax import lax
from jax.sharding import PartitionSpec as P

BLK = 4
CLASSES = 8
STEPS = 2


TIME_STEP = 0.15
SIGMA_LONG = 1.0
SIGMA_CROSS = 0.3
SLOPES = (8.0, -8.0, 6.0, 5.0, -5.0, -3.0)
MIDDLES = (0.2, 0.4, 0.3, 0.5, 0.6, 0.5)
RATES = (3.0, 0.5, 1.0, 0.8, 0.3, 0.1)
OPACITY = (0.012, 0.01)


def swapped(x, axis, bit):
    return lax.ppermute(x, axis, [(i, i ^ 1 << bit) for i in range(lax.axis_size(axis))])


def padded_2(x, sides, width):
    for axis, dim in sides:
        count, length = (lax.axis_size(axis), x.shape[dim])
        up = [(i, (i + 1) % count) for i in range(count - 1)]
        down = [(j, i) for i, j in up]
        last = lax.slice_in_dim(x, length - width, length, axis=dim)
        leading = lax.slice_in_dim(x, 0, width, axis=dim)
        before = lax.ppermute(last, axis, up)
        after = lax.ppermute(leading, axis, down)
        x = jnp.concatenate([before, x, after], axis=dim)
    return x


def spread_blocks(stacked):
    fields, first, second, third = stacked.shape
    columns = third * BLK
    onehot = (jnp.arange(columns)[None, :] // BLK == jnp.arange(third)[:, None]).astype(jnp.float32)
    along = jnp.dot(
        stacked.reshape(fields * first * second, third),
        onehot,
        precision=lax.Precision.HIGHEST,
        preferred_element_type=jnp.float32,
    )
    along = along.reshape(fields, first, 1, second, 1, columns)
    wide = jnp.broadcast_to(along, (fields, first, BLK, second, BLK, columns))
    return wide.reshape(fields, first * BLK, second * BLK, columns)


def block_fields(tissue, fiber):
    kind = fiber.astype(jnp.float32)
    polar = math.pi * (kind + 0.5) / CLASSES
    azimuth = 2.3 * kind
    along_x = jnp.cos(polar)
    along_y = jnp.sin(polar) * jnp.cos(azimuth)
    along_z = jnp.sin(polar) * jnp.sin(azimuth)
    spread = SIGMA_LONG - SIGMA_CROSS
    parts = [
        tissue.astype(jnp.float32),
        SIGMA_CROSS + spread * along_x * along_x,
        SIGMA_CROSS + spread * along_y * along_y,
        SIGMA_CROSS + spread * along_z * along_z,
        spread * along_x * along_y,
        spread * along_x * along_z,
        spread * along_y * along_z,
    ]
    wide = spread_blocks(jnp.stack(parts))
    return (wide[0], tuple((wide[k] for k in range(1, 7))))


def diffuse(padded, comps):
    centre = padded[1:-1, 1:-1, 1:-1]
    second_x = padded[2:, 1:-1, 1:-1] - 2.0 * centre + padded[:-2, 1:-1, 1:-1]
    second_y = padded[1:-1, 2:, 1:-1] - 2.0 * centre + padded[1:-1, :-2, 1:-1]
    second_z = padded[1:-1, 1:-1, 2:] - 2.0 * centre + padded[1:-1, 1:-1, :-2]
    cross_xy = 0.25 * (
        padded[2:, 2:, 1:-1]
        - padded[2:, :-2, 1:-1]
        - padded[:-2, 2:, 1:-1]
        + padded[:-2, :-2, 1:-1]
    )
    cross_xz = 0.25 * (
        padded[2:, 1:-1, 2:]
        - padded[2:, 1:-1, :-2]
        - padded[:-2, 1:-1, 2:]
        + padded[:-2, 1:-1, :-2]
    )
    cross_yz = 0.25 * (
        padded[1:-1, 2:, 2:]
        - padded[1:-1, 2:, :-2]
        - padded[1:-1, :-2, 2:]
        + padded[1:-1, :-2, :-2]
    )
    dxx, dyy, dzz, dxy, dxz, dyz = comps
    return (
        dxx * second_x
        + dyy * second_y
        + dzz * second_z
        + 2.0 * (dxy * cross_xy + dxz * cross_xz + dyz * cross_yz)
    )


def ionic(voltage, gates, calcium):
    fresh = []
    for k in range(6):
        steady = jax.nn.sigmoid(SLOPES[k] * (voltage - MIDDLES[k]))
        fresh.append(steady + (gates[k] - steady) * math.exp(-TIME_STEP * RATES[k]))
    current = (
        2.0 * fresh[0] * fresh[0] * fresh[0] * fresh[1] * (voltage - 1.2)
        + fresh[2] * fresh[2] * (voltage + 0.1)
        + 0.6 * fresh[3] * fresh[4] * (voltage - 0.9)
        + 0.2 * (1.0 + fresh[5]) * (voltage - 0.05)
    )
    volt_next = voltage - TIME_STEP * current
    calc_next = calcium + TIME_STEP * (1.5 * fresh[3] * fresh[4] * (1.0 - calcium) - 0.8 * calcium)
    return (volt_next, fresh, calc_next)


def emission(field, tissue_float, which):
    alpha = OPACITY[which] * tissue_float * jax.nn.sigmoid(6.0 * (field - 0.4))
    red = jax.nn.sigmoid(5.0 * (field - 0.5))
    green = jnp.exp(-6.0 * (field - 0.5) * (field - 0.5))
    return (alpha, (red, green, 1.0 - red))


def march(alpha, colours):
    through = jnp.cumprod(1.0 - alpha, axis=0)
    before = jnp.concatenate([jnp.ones_like(through[:1]), through[:-1]], axis=0)
    weight = before * alpha
    colour = jnp.stack([jnp.sum(weight * item, axis=0) for item in colours])
    return (colour, through[-1])


def composite(colour, through):
    index = lax.axis_index("depth")
    groups = lax.axis_size("depth")
    rows = colour.shape[2]
    width = colour.shape[3] // groups
    mine_colour = colour.reshape(2, 3, rows, groups, width)
    mine_through = through.reshape(2, 1, rows, groups, width)
    for level in range(groups.bit_length() - 1):
        count = mine_colour.shape[3] // 2
        front = index >> level & 1 == 0
        paired_colour = mine_colour.reshape(2, 3, rows, count, 2, width)
        paired_through = mine_through.reshape(2, 1, rows, count, 2, width)
        keep_colour = jnp.where(front, paired_colour[:, :, :, :, 0], paired_colour[:, :, :, :, 1])
        give_colour = jnp.where(front, paired_colour[:, :, :, :, 1], paired_colour[:, :, :, :, 0])
        keep_through = jnp.where(
            front, paired_through[:, :, :, :, 0], paired_through[:, :, :, :, 1]
        )
        give_through = jnp.where(
            front, paired_through[:, :, :, :, 1], paired_through[:, :, :, :, 0]
        )
        other_colour, other_through = swapped((give_colour, give_through), "depth", level)
        mine_colour = jnp.where(
            front,
            keep_colour + keep_through * other_colour,
            other_colour + other_through * keep_colour,
        )
        mine_through = keep_through * other_through
    return (mine_colour[:, :, :, 0], mine_through[:, :, :, 0])


def per_device(states, tissue, fiber):
    tissue_float, comps = block_fields(tissue, fiber)
    voltage = states[0]
    gates = [states[k] for k in range(1, 7)]
    calcium = states[7]
    pieces = []
    for step in range(STEPS):
        rimmed = padded_2(voltage * tissue_float, (("depth", 0), ("area", 1)), 1)
        padded = jnp.pad(rimmed, ((0, 0), (0, 0), (1, 1)))
        diffused = voltage + TIME_STEP * diffuse(padded, comps)
        volt_next, fresh, calc_next = ionic(diffused, gates, calcium)
        keep = 1.0 - tissue_float
        voltage = tissue_float * volt_next + keep * voltage
        gates = [tissue_float * item + keep * old for item, old in zip(fresh, gates)]
        calcium = tissue_float * calc_next + keep * calcium
        colours = []
        throughs = []
        for which, field in enumerate((voltage, calcium)):
            alpha, tints = emission(field, tissue_float, which)
            colour, through = march(alpha, tints)
            colours.append(colour)
            throughs.append(through[None])
        pieces.append(composite(jnp.stack(colours), jnp.stack(throughs)))
    colour_all = jnp.stack([item[0] for item in pieces])
    through_all = jnp.stack([item[1] for item in pieces])
    images = jnp.concatenate([colour_all, 1.0 - through_all], axis=2)
    final_states = jnp.stack([voltage] + gates + [calcium])
    return (final_states, images)


def solution(mesh):
    return jax.shard_map(
        per_device,
        mesh=mesh,
        in_specs=(
            P(None, "depth", "area", None),
            P("depth", "area", None),
            P("depth", "area", None),
        ),
        out_specs=(P(None, "depth", "area", None), P(None, None, None, "area", "depth")),
        check_vma=False,
    )
```

profile of v0, /device:TPU:0, one launch (start us, length us, event | category | flops | bytes accessed | tf_op | source)
XLA Modules:
  0.0 108.9 jit_solution(6041200521462315617)
XLA Ops:
  0.6 1.0 multiply_multiply_fusion.7
  1.8 0.7 convert_element_type.10
  2.7 0.4 fusion.105
  3.1 0.2 fusion.157
  3.5 0.3 broadcast_in_dim.34
  3.8 1.2 %bitcast_multiply_fusion.9 = f32[16,16,768]{2,1,0:T(8,128)S(1)} fusion(f32[16,16,768]{2,1,0:T(8,128)S(1)} %broadcast_in_dim.34, f32[8,16,16,768]{3,2,1,0:T(8,128)} %param.3), kind=kLoop, calls=%fused_computation.167 | loop fusion | flops 196608 | bytes 2359296 | tf_op jit(solution)/shard_map/mul | solution.py:175
  5.0 1.3 %collective-permute-start = (f32[1,16,768]{2,1,0:T(8,128)S(1)}, f32[1,16,768]{2,1,0:T(8,128)S(1)}, u32[]{:S(2)}, u32[]{:S(2)}) collective-permute-start(f32[1,16,768]{2,1,0:T(8,128)S(1)} %get-tuple-element.55), channel_id=1, source_target_pairs={{8,0},{16,8},{24,16},{9,1},{17,9},{25,17},{10,2},{18,10},{26,18},{... | collective-permute-start | bytes 147464 | tf_op jit(solution)/shard_map/ppermute | solution.py:34
  6.3 5.5 %collective-permute-start.1 = (f32[1,16,768]{2,1,0:T(8,128)S(1)}, f32[1,16,768]{2,1,0:T(8,128)S(1)}, u32[]{:S(2)}, u32[]{:S(2)}) collective-permute-start(f32[1,16,768]{2,1,0:T(8,128)S(1)} %get-tuple-element.54), channel_id=1, source_target_pairs={{0,8},{8,16},{16,24},{1,9},{9,17},{17,25},{2,10},{10,18},{18,26},{... | collective-permute-start | bytes 147464 | tf_op jit(solution)/shard_map/ppermute | solution.py:33
  12.0 1.6 %collective-permute-done.1 = f32[1,16,768]{2,1,0:T(8,128)S(1)} collective-permute-done((f32[1,16,768]{2,1,0:T(8,128)S(1)}, f32[1,16,768]{2,1,0:T(8,128)S(1)}, u32[]{:S(2)}, u32[]{:S(2)}) %collective-permute-start.1) | collective-permute-done | bytes 49184 | tf_op jit(solution)/shard_map/ppermute | solution.py:33
  13.6 1.3 %collective-permute-start.2 = (f32[18,1,768]{2,1,0:T(1,128)S(1)}, f32[18,1,768]{2,1,0:T(1,128)S(1)}, u32[]{:S(2)}, u32[]{:S(2)}) collective-permute-start(f32[18,1,768]{2,1,0:T(1,128)S(1)} %get-tuple-element.51), channel_id=1, source_target_pairs={{1,0},{2,1},{3,2},{4,3},{5,4},{6,5},{7,6},{9,8},{10,9},{11,10},{12... | collective-permute-start | bytes 165896 | tf_op jit(solution)/shard_map/ppermute | solution.py:34
  14.9 3.0 %collective-permute-start.3 = (f32[18,1,768]{2,1,0:T(1,128)S(1)}, f32[18,1,768]{2,1,0:T(1,128)S(1)}, u32[]{:S(2)}, u32[]{:S(2)}) collective-permute-start(f32[18,1,768]{2,1,0:T(1,128)S(1)} %get-tuple-element.50), channel_id=1, source_target_pairs={{0,1},{1,2},{2,3},{3,4},{4,5},{5,6},{6,7},{8,9},{9,10},{10,11},{11... | collective-permute-start | bytes 165896 | tf_op jit(solution)/shard_map/ppermute | solution.py:33
  18.2 1.2 %broadcast_in_dim.36 = f32[16,16,768]{2,1,0:T(8,128)} reshape(f32[4,4,4,4,768]{4,3,2,1,0:T(4,128)S(1)} %broadcast_in_dim.35) | data formatting | bytes 1572864 | tf_op jit(solution)/shard_map/broadcast_in_dim | solution.py:50
  19.5 1.2 %broadcast_in_dim.38 = f32[16,16,768]{2,1,0:T(8,128)} reshape(f32[4,4,4,4,768]{4,3,2,1,0:T(4,128)S(1)} %broadcast_in_dim.37) | data formatting | bytes 1572864 | tf_op jit(solution)/shard_map/broadcast_in_dim | solution.py:50
  20.8 1.2 %broadcast_in_dim.40 = f32[16,16,768]{2,1,0:T(8,128)} reshape(f32[4,4,4,4,768]{4,3,2,1,0:T(4,128)S(1)} %broadcast_in_dim.39) | data formatting | bytes 1572864 | tf_op jit(solution)/shard_map/broadcast_in_dim | solution.py:50
  22.1 1.2 %broadcast_in_dim.42 = f32[16,16,768]{2,1,0:T(8,128)} reshape(f32[4,4,4,4,768]{4,3,2,1,0:T(4,128)S(1)} %broadcast_in_dim.41) | data formatting | bytes 1572864 | tf_op jit(solution)/shard_map/broadcast_in_dim | solution.py:50
  23.5 1.2 %broadcast_in_dim.44 = f32[16,16,768]{2,1,0:T(8,128)} reshape(f32[4,4,4,4,768]{4,3,2,1,0:T(4,128)S(1)} %broadcast_in_dim.43) | data formatting | bytes 1572864 | tf_op jit(solution)/shard_map/broadcast_in_dim | solution.py:50
  24.8 1.2 %broadcast_in_dim.46 = f32[16,16,768]{2,1,0:T(8,128)} reshape(f32[4,4,4,4,768]{4,3,2,1,0:T(4,128)S(1)} %broadcast_in_dim.45) | data formatting | bytes 1572864 | tf_op jit(solution)/shard_map/broadcast_in_dim | solution.py:50
  26.2 0.8 select_maximum_fusion.4
  27.1 0.2 copy-done.12
  27.3 0.3 copy-done.14
  27.6 0.3 copy-done.4
  28.1 0.2 copy-done.8
  28.3 7.1 %fusion.149 = (f32[16,16,768]{2,1,0:T(8,128)S(1)}, f32[16,16,768]{2,1,0:T(8,128)S(1)}, f32[16,16,768]{2,1,0:T(8,128)}, f32[16,16,768]{2,1,0:T(8,128)}, f32[16,16,768]{2,1,0:T(8,128)S(1)}) fusion(f32[16,16,768]{2,1,0:T(8,128)S(1)} %broadcast_in_dim.34, f32[8,16,16,768]{3,2,1,0:T(8,128)} %param.3, f32[16,16,768]{2,1,0:T(8,128)S(1)} %copy-done.14, ...), kind=kLoop, calls=%fused_computation.319 | loop fusion | flops 21430272 | bytes 28409856 | tf_op jit(solution)/shard_map/mul | solution.py:175
  35.5 1.3 %collective-permute-start.4 = (f32[1,16,768]{2,1,0:T(8,128)S(1)}, f32[1,16,768]{2,1,0:T(8,128)S(1)}, u32[]{:S(2)}, u32[]{:S(2)}) collective-permute-start(f32[1,16,768]{2,1,0:T(8,128)S(1)} %get-tuple-element.53), channel_id=1, source_target_pairs={{8,0},{16,8},{24,16},{9,1},{17,9},{25,17},{10,2},{18,10},{26,18},{... | collective-permute-start | bytes 147464 | tf_op jit(solution)/shard_map/ppermute | solution.py:34
  36.8 5.4 %collective-permute-start.5 = (f32[1,16,768]{2,1,0:T(8,128)S(1)}, f32[1,16,768]{2,1,0:T(8,128)S(1)}, u32[]{:S(2)}, u32[]{:S(2)}) collective-permute-start(f32[1,16,768]{2,1,0:T(8,128)S(1)} %get-tuple-element.52), channel_id=1, source_target_pairs={{0,8},{8,16},{16,24},{1,9},{9,17},{17,25},{2,10},{10,18},{18,26},{... | collective-permute-start | bytes 147464 | tf_op jit(solution)/shard_map/ppermute | solution.py:33
  42.3 0.4 fusion.98
  42.9 1.3 %collective-permute-done.5 = f32[1,16,768]{2,1,0:T(8,128)S(1)} collective-permute-done((f32[1,16,768]{2,1,0:T(8,128)S(1)}, f32[1,16,768]{2,1,0:T(8,128)S(1)}, u32[]{:S(2)}, u32[]{:S(2)}) %collective-permute-start.5) | collective-permute-done | bytes 49184 | tf_op jit(solution)/shard_map/ppermute | solution.py:33
  44.2 1.3 %collective-permute-start.6 = (f32[18,1,768]{2,1,0:T(1,128)S(1)}, f32[18,1,768]{2,1,0:T(1,128)S(1)}, u32[]{:S(2)}, u32[]{:S(2)}) collective-permute-start(f32[18,1,768]{2,1,0:T(1,128)S(1)} %get-tuple-element.47), channel_id=1, source_target_pairs={{1,0},{2,1},{3,2},{4,3},{5,4},{6,5},{7,6},{9,8},{10,9},{11,10},{12... | collective-permute-start | bytes 165896 | tf_op jit(solution)/shard_map/ppermute | solution.py:34
  45.5 3.2 %collective-permute-start.7 = (f32[18,1,768]{2,1,0:T(1,128)S(1)}, f32[18,1,768]{2,1,0:T(1,128)S(1)}, u32[]{:S(2)}, u32[]{:S(2)}) collective-permute-start(f32[18,1,768]{2,1,0:T(1,128)S(1)} %get-tuple-element.46), channel_id=1, source_target_pairs={{0,1},{1,2},{2,3},{3,4},{4,5},{5,6},{6,7},{8,9},{9,10},{10,11},{11... | collective-permute-start | bytes 165896 | tf_op jit(solution)/shard_map/ppermute | solution.py:33
  48.8 0.6 collective-permute-done.7
  49.7 0.8 select_maximum_fusion
  50.6 0.2 copy-done.2
  50.9 0.2 copy-done.3
  51.1 0.2 copy-done.5
  51.3 0.2 copy-done.7
  51.6 0.2 copy-done.9
  52.0 8.0 %bitcast_dynamic-update-slice_fusion.7 = (f32[8,16,16,768]{3,2,1,0:T(8,128)}, f32[16,16,768]{2,1,0:T(8,128)}, f32[16,16,768]{2,1,0:T(8,128)S(1)}) fusion(f32[16,16,768]{2,1,0:T(8,128)S(1)} %copy-done.1, f32[16,16,768]{2,1,0:T(8,128)S(1)} %broadcast_in_dim.34, f32[8,16,16,768]{3,2,1,0:T(8,128)} %param.3, f32[16,16,768]{2,1,0:T(8,128)S(1)} %get-tuple-element.43, ...), kind=kLoop, calls=%fused_computation.135 | loop fusion | flops 31064064 | bytes 29196288
  60.0 1.5 %bitcast_dynamic-update-slice_fusion.6 = f32[8,16,16,768]{3,2,1,0:T(8,128)} fusion(f32[8,16,16,768]{3,2,1,0:T(8,128)} %get-tuple-element.36, f32[16,16,768]{2,1,0:T(8,128)S(1)} %broadcast_in_dim.34, f32[16,16,768]{2,1,0:T(8,128)S(1)} %get-tuple-element.38, f32[8,16,16,768]{3,2,1,0:T(8,128)S(1)} %bitcast.306, f32[16,16,768]{2,1,0:T(8,128)S(1)} %get-tuple-element.43), kind=kLoop, calls=%fused_computation.134 | loop fusion | flops 4521984 | bytes 3932160
  61.6 1.5 %bitcast_dynamic-update-slice_fusion.5 = f32[8,16,16,768]{3,2,1,0:T(8,128)} fusion(f32[8,16,16,768]{3,2,1,0:T(8,128)} %bitcast_dynamic-update-slice_fusion.6, f32[16,16,768]{2,1,0:T(8,128)S(1)} %broadcast_in_dim.34, f32[16,16,768]{2,1,0:T(8,128)S(1)} %get-tuple-element.38, f32[8,16,16,768]{3,2,1,0:T(8,128)S(1)} %bitcast.306, ...), kind=kLoop, calls=%fused_computation.133 | loop fusion | flops 4521984 | bytes 3932160
  63.1 1.5 %bitcast_dynamic-update-slice_fusion.4 = f32[8,16,16,768]{3,2,1,0:T(8,128)} fusion(f32[8,16,16,768]{3,2,1,0:T(8,128)} %bitcast_dynamic-update-slice_fusion.5, f32[16,16,768]{2,1,0:T(8,128)S(1)} %broadcast_in_dim.34, f32[16,16,768]{2,1,0:T(8,128)S(1)} %get-tuple-element.38, f32[8,16,16,768]{3,2,1,0:T(8,128)S(1)} %bitcast.306, ...), kind=kLoop, calls=%fused_computation.132 | loop fusion | flops 4521984 | bytes 3932160
  64.6 1.3 %bitcast_dynamic-update-slice_fusion.3 = f32[8,16,16,768]{3,2,1,0:T(8,128)} fusion(f32[8,16,16,768]{3,2,1,0:T(8,128)} %bitcast_dynamic-update-slice_fusion.4, f32[16,16,768]{2,1,0:T(8,128)S(1)} %broadcast_in_dim.34, f32[16,16,768]{2,1,0:T(8,128)S(1)} %get-tuple-element.38, f32[8,16,16,768]{3,2,1,0:T(8,128)S(1)} %bitcast.306, f32[16,16,768]{2,1,0:T(8,128)S(1)} %copy-done.2), kind=kLoop, calls=%fused_computation.131 | loop fusion | flops 2949120 | bytes 3932160
  66.0 1.3 %bitcast_dynamic-update-slice_fusion.2 = f32[8,16,16,768]{3,2,1,0:T(8,128)} fusion(f32[8,16,16,768]{3,2,1,0:T(8,128)} %bitcast_dynamic-update-slice_fusion.3, f32[16,16,768]{2,1,0:T(8,128)S(1)} %broadcast_in_dim.34, f32[16,16,768]{2,1,0:T(8,128)S(1)} %get-tuple-element.38, f32[8,16,16,768]{3,2,1,0:T(8,128)S(1)} %bitcast.306, f32[16,16,768]{2,1,0:T(8,128)S(1)} %copy-done.3), kind=kLoop, calls=%fused_computation.130 | loop fusion | flops 2949120 | bytes 3932160
  67.3 1.5 %bitcast_dynamic-update-slice_fusion.1 = f32[8,16,16,768]{3,2,1,0:T(8,128)} fusion(f32[8,16,16,768]{3,2,1,0:T(8,128)} %bitcast_dynamic-update-slice_fusion.2, f32[16,16,768]{2,1,0:T(8,128)S(1)} %broadcast_in_dim.34, f32[16,16,768]{2,1,0:T(8,128)S(1)} %get-tuple-element.38, f32[8,16,16,768]{3,2,1,0:T(8,128)S(1)} %bitcast.306, ...), kind=kLoop, calls=%fused_computation.129 | loop fusion | flops 4521984 | bytes 3932160
  68.8 2.1 %bitcast_dynamic-update-slice_fusion = (f32[8,16,16,768]{3,2,1,0:T(8,128)}, f32[16,16,768]{2,1,0:T(8,128)S(1)}, f32[16,16,768]{2,1,0:T(8,128)S(1)}) fusion(f32[8,16,16,768]{3,2,1,0:T(8,128)} %bitcast_dynamic-update-slice_fusion.1, f32[16,16,768]{2,1,0:T(8,128)S(1)} %broadcast_in_dim.34, f32[8,16,16,768]{3,2,1,0:T(8,128)S(1)} %bitcast.306, ...), kind=kLoop, calls=%fused_computation.119 | loop fusion | flops 8847360 | bytes 7864320 | tf_op jit(solution)/shard_map/stack | solution.py:194
  70.9 0.4 fusion.96
  71.3 0.4 fusion.92
  71.8 0.4 copy-done.17
  72.2 0.5 copy-done.15
  72.7 0.4 fusion.94
  73.2 0.6 slice-done.2
  74.1 2.9 %multiply_reduce_fusion.7 = (f32[16,768]{1,0:T(8,128)S(1)}, f32[16,768]{1,0:T(8,128)S(1)}, f32[16,768]{1,0:T(8,128)S(1)}, f32[16,768]{1,0:T(8,128)S(1)}, f32[16,...) fusion(f32[16,16,768]{2,1,0:T(8,128)S(1)} %copy-done.1, ...), kind=kLoop, calls=%fused_computation.190 | loop fusion | flops 16760832 | bytes 7471104 | tf_op jit(solution)/shard_map/reduce_sum | solution.py:134
  78.0 0.4 fusion.156
  78.5 3.3 %collective-permute-start.8 = (f32[2,3,16,2,192]{4,3,2,1,0:T(2,128)S(1)}, f32[2,3,16,2,192]{4,3,2,1,0:T(2,128)S(1)}, u32[]{:S(2)}, u32[]{:S(2)}) collective-permute-start(f32[2,3,16,2,192]{4,3,2,1,0:T(2,128)S(1)} %bitcast.312), channel_id=1, source_target_pairs={{0,8},{8,0},{16,24},{24,16},{1,9},{9,1},{17,25},{25,17},{2,10},{10... | collective-permute-start | bytes 442376 | tf_op jit(solution)/shard_map/ppermute | solution.py:23
  83.4 2.1 %collective-permute-start.12 = (f32[2,3,16,2,192]{4,3,2,1,0:T(2,128)S(1)}, f32[2,3,16,2,192]{4,3,2,1,0:T(2,128)S(1)}, u32[]{:S(2)}, u32[]{:S(2)}) collective-permute-start(f32[2,3,16,2,192]{4,3,2,1,0:T(2,128)S(1)} %select_bitcast_fusion), channel_id=1, source_target_pairs={{0,8},{8,0},{16,24},{24,16},{1,9},{9,1},{17,25},{25,17},{2,10},{10... | collective-permute-start | bytes 442376 | tf_op jit(solution)/shard_map/ppermute | solution.py:23
  86.0 1.7 %collective-permute-done.9 = f32[2,1,16,2,192]{4,1,3,2,0:T(1,128)S(1)} collective-permute-done((f32[2,1,16,2,192]{4,1,3,2,0:T(1,128)S(1)}, f32[2,1,16,2,192]{4,1,3,2,0:T(1,128)S(1)}, u32[]{:S(2)}, u32[]{:S(2)}) %collective-permute-start.9) | collective-permute-done | bytes 49184 | tf_op jit(solution)/shard_map/ppermute | solution.py:23
  87.9 4.5 %collective-permute-start.11 = (f32[2,1,16,1,192]{4,1,3,2,0:T(1,128)S(1)}, f32[2,1,16,1,192]{4,1,3,2,0:T(1,128)S(1)}, u32[]{:S(2)}, u32[]{:S(2)}) collective-permute-start(f32[2,1,16,1,192]{4,1,3,2,0:T(1,128)S(1)} %fusion.125), channel_id=1, source_target_pairs={{0,16},{8,24},{16,0},{24,8},{1,17},{9,25},{17,1},{25,9},{2,18},{10... | collective-permute-start | bytes 73736 | tf_op jit(solution)/shard_map/ppermute | solution.py:23
  92.4 0.9 collective-permute-done.13
  93.6 4.5 %collective-permute-start.15 = (f32[2,1,16,1,192]{4,1,3,2,0:T(1,128)S(1)}, f32[2,1,16,1,192]{4,1,3,2,0:T(1,128)S(1)}, u32[]{:S(2)}, u32[]{:S(2)}) collective-permute-start(f32[2,1,16,1,192]{4,1,3,2,0:T(1,128)S(1)} %fusion.126), channel_id=1, source_target_pairs={{0,16},{8,24},{16,0},{24,8},{1,17},{9,25},{17,1},{25,9},{2,18},{10... | collective-permute-start | bytes 73736 | tf_op jit(solution)/shard_map/ppermute | solution.py:23
  98.2 1.9 %collective-permute-done.15 = f32[2,1,16,1,192]{4,1,3,2,0:T(1,128)S(1)} collective-permute-done((f32[2,1,16,1,192]{4,1,3,2,0:T(1,128)S(1)}, f32[2,1,16,1,192]{4,1,3,2,0:T(1,128)S(1)}, u32[]{:S(2)}, u32[]{:S(2)}) %collective-permute-start.15) | collective-permute-done | bytes 24608 | tf_op jit(solution)/shard_map/ppermute | solution.py:23
  100.7 1.9 %collective-permute-start.10 = (f32[2,3,16,1,192]{4,3,2,1,0:T(1,128)S(1)}, f32[2,3,16,1,192]{4,3,2,1,0:T(1,128)S(1)}, u32[]{:S(2)}, u32[]{:S(2)}) collective-permute-start(f32[2,3,16,1,192]{4,3,2,1,0:T(1,128)S(1)} %fusion.120), channel_id=1, source_target_pairs={{0,16},{8,24},{16,0},{24,8},{1,17},{9,25},{17,1},{25,9},{2,18},{10... | collective-permute-start | bytes 221192 | tf_op jit(solution)/shard_map/ppermute | solution.py:23
  103.1 0.3 collective-permute-start.14
  103.3 2.8 %collective-permute-done.10 = f32[2,3,16,1,192]{4,3,2,1,0:T(1,128)S(1)} collective-permute-done((f32[2,3,16,1,192]{4,3,2,1,0:T(1,128)S(1)}, f32[2,3,16,1,192]{4,3,2,1,0:T(1,128)S(1)}, u32[]{:S(2)}, u32[]{:S(2)}) %collective-permute-start.10) | collective-permute-done | bytes 73760 | tf_op jit(solution)/shard_map/ppermute | solution.py:23
  106.3 1.4 %collective-permute-done.14 = f32[2,3,16,1,192]{4,3,2,1,0:T(1,128)S(1)} collective-permute-done((f32[2,3,16,1,192]{4,3,2,1,0:T(1,128)S(1)}, f32[2,3,16,1,192]{4,3,2,1,0:T(1,128)S(1)}, u32[]{:S(2)}, u32[]{:S(2)}) %collective-permute-start.14) | collective-permute-done | bytes 73760 | tf_op jit(solution)/shard_map/ppermute | solution.py:23
  108.1 0.7 copy.39
  (137 shorter events, 8.1 us)
Async XLA Ops:
  5.0 6.9 %collective-permute-start = (f32[1,16,768]{2,1,0:T(8,128)S(1)}, f32[1,16,768]{2,1,0:T(8,128)S(1)}, u32[]{:S(2)}, u32[]{:S(2)}) collective-permute-start(f32[1,16,768]{2,1,0:T(8,128)S(1)} %get-tuple-element.55), channel_id=1, source_target_pairs={{8,0},{16,8},{24,16},{9,1},{17,9},{25,17},{10,2},{18,10},{26,18},{... | collective-permute-start | bytes 147464 | tf_op jit(solution)/shard_map/ppermute | solution.py:34
  6.3 7.2 %collective-permute-start.1 = (f32[1,16,768]{2,1,0:T(8,128)S(1)}, f32[1,16,768]{2,1,0:T(8,128)S(1)}, u32[]{:S(2)}, u32[]{:S(2)}) collective-permute-start(f32[1,16,768]{2,1,0:T(8,128)S(1)} %get-tuple-element.54), channel_id=1, source_target_pairs={{0,8},{8,16},{16,24},{1,9},{9,17},{17,25},{2,10},{10,18},{18,26},{... | collective-permute-start | bytes 147464 | tf_op jit(solution)/shard_map/ppermute | solution.py:33
  13.6 12.3 %collective-permute-start.2 = (f32[18,1,768]{2,1,0:T(1,128)S(1)}, f32[18,1,768]{2,1,0:T(1,128)S(1)}, u32[]{:S(2)}, u32[]{:S(2)}) collective-permute-start(f32[18,1,768]{2,1,0:T(1,128)S(1)} %get-tuple-element.51), channel_id=1, source_target_pairs={{1,0},{2,1},{3,2},{4,3},{5,4},{6,5},{7,6},{9,8},{10,9},{11,10},{12... | collective-permute-start | bytes 165896 | tf_op jit(solution)/shard_map/ppermute | solution.py:34
  14.9 11.0 %collective-permute-start.3 = (f32[18,1,768]{2,1,0:T(1,128)S(1)}, f32[18,1,768]{2,1,0:T(1,128)S(1)}, u32[]{:S(2)}, u32[]{:S(2)}) collective-permute-start(f32[18,1,768]{2,1,0:T(1,128)S(1)} %get-tuple-element.50), channel_id=1, source_target_pairs={{0,1},{1,2},{2,3},{3,4},{4,5},{5,6},{6,7},{8,9},{9,10},{10,11},{11... | collective-permute-start | bytes 165896 | tf_op jit(solution)/shard_map/ppermute | solution.py:33
  26.0 1.1 %copy-start.10 = (f32[16,16,768]{2,1,0:T(8,128)S(1)}, f32[16,16,768]{2,1,0:T(8,128)}, u32[]{:S(2)}) copy-start(f32[16,16,768]{2,1,0:T(8,128)} %broadcast_in_dim.42) | copy-start | bytes 2359300
  26.0 1.4 %copy-start.12 = (f32[16,16,768]{2,1,0:T(8,128)S(1)}, f32[16,16,768]{2,1,0:T(8,128)}, u32[]{:S(2)}) copy-start(f32[16,16,768]{2,1,0:T(8,128)} %broadcast_in_dim.44) | copy-start | bytes 2359300
  26.0 1.6 %copy-start.14 = (f32[16,16,768]{2,1,0:T(8,128)S(1)}, f32[16,16,768]{2,1,0:T(8,128)}, u32[]{:S(2)}) copy-start(f32[16,16,768]{2,1,0:T(8,128)} %broadcast_in_dim.46) | copy-start | bytes 2359300
  26.2 1.7 %copy-start.4 = (f32[16,16,768]{2,1,0:T(8,128)S(1)}, f32[16,16,768]{2,1,0:T(8,128)}, u32[]{:S(2)}) copy-start(f32[16,16,768]{2,1,0:T(8,128)} %broadcast_in_dim.36) | copy-start | bytes 2359300
  26.2 1.9 %copy-start.6 = (f32[16,16,768]{2,1,0:T(8,128)S(1)}, f32[16,16,768]{2,1,0:T(8,128)}, u32[]{:S(2)}) copy-start(f32[16,16,768]{2,1,0:T(8,128)} %broadcast_in_dim.38) | copy-start | bytes 2359300
  26.2 2.1 %copy-start.8 = (f32[16,16,768]{2,1,0:T(8,128)S(1)}, f32[16,16,768]{2,1,0:T(8,128)}, u32[]{:S(2)}) copy-start(f32[16,16,768]{2,1,0:T(8,128)} %broadcast_in_dim.40) | copy-start | bytes 2359300
  35.5 6.8 %copy-start = (f32[16,16,768]{2,1,0:T(8,128)}, f32[16,16,768]{2,1,0:T(8,128)S(1)}, u32[]{:S(2)}) copy-start(f32[16,16,768]{2,1,0:T(8,128)S(1)} %get-tuple-element.40) | copy-start | bytes 2359300
  35.5 7.4 %collective-permute-start.4 = (f32[1,16,768]{2,1,0:T(8,128)S(1)}, f32[1,16,768]{2,1,0:T(8,128)S(1)}, u32[]{:S(2)}, u32[]{:S(2)}) collective-permute-start(f32[1,16,768]{2,1,0:T(8,128)S(1)} %get-tuple-element.53), channel_id=1, source_target_pairs={{8,0},{16,8},{24,16},{9,1},{17,9},{25,17},{10,2},{18,10},{26,18},{... | collective-permute-start | bytes 147464 | tf_op jit(solution)/shard_map/ppermute | solution.py:34
  36.8 7.3 %collective-permute-start.5 = (f32[1,16,768]{2,1,0:T(8,128)S(1)}, f32[1,16,768]{2,1,0:T(8,128)S(1)}, u32[]{:S(2)}, u32[]{:S(2)}) collective-permute-start(f32[1,16,768]{2,1,0:T(8,128)S(1)} %get-tuple-element.52), channel_id=1, source_target_pairs={{0,8},{8,16},{16,24},{1,9},{9,17},{17,25},{2,10},{10,18},{18,26},{... | collective-permute-start | bytes 147464 | tf_op jit(solution)/shard_map/ppermute | solution.py:33
  42.7 6.1 %copy-start.16 = (f32[16,16,768]{2,1,0:T(8,128)}, f32[16,16,768]{2,1,0:T(8,128)S(1)}, u32[]{:S(2)}) copy-start(f32[16,16,768]{2,1,0:T(8,128)S(1)} %fusion.98) | copy-start | bytes 2359300
  44.2 4.6 %collective-permute-start.6 = (f32[18,1,768]{2,1,0:T(1,128)S(1)}, f32[18,1,768]{2,1,0:T(1,128)S(1)}, u32[]{:S(2)}, u32[]{:S(2)}) collective-permute-start(f32[18,1,768]{2,1,0:T(1,128)S(1)} %get-tuple-element.47), channel_id=1, source_target_pairs={{1,0},{2,1},{3,2},{4,3},{5,4},{6,5},{7,6},{9,8},{10,9},{11,10},{12... | collective-permute-start | bytes 165896 | tf_op jit(solution)/shard_map/ppermute | solution.py:34
  45.5 3.9 %collective-permute-start.7 = (f32[18,1,768]{2,1,0:T(1,128)S(1)}, f32[18,1,768]{2,1,0:T(1,128)S(1)}, u32[]{:S(2)}, u32[]{:S(2)}) collective-permute-start(f32[18,1,768]{2,1,0:T(1,128)S(1)} %get-tuple-element.46), channel_id=1, source_target_pairs={{0,1},{1,2},{2,3},{3,4},{4,5},{5,6},{6,7},{8,9},{9,10},{10,11},{11... | collective-permute-start | bytes 165896 | tf_op jit(solution)/shard_map/ppermute | solution.py:33
  48.7 1.8 %copy-start.13 = (f32[16,16,768]{2,1,0:T(8,128)S(1)}, f32[16,16,768]{2,1,0:T(8,128)}, u32[]{:S(2)}) copy-start(f32[16,16,768]{2,1,0:T(8,128)} %broadcast_in_dim.44) | copy-start | bytes 2359300
  49.4 1.2 %copy-start.1 = (f32[16,16,768]{2,1,0:T(8,128)S(1)}, f32[16,16,768]{2,1,0:T(8,128)}, u32[]{:S(2)}) copy-start(f32[16,16,768]{2,1,0:T(8,128)} %copy-done) | copy-start | bytes 2359300
  49.4 1.4 %copy-start.2 = (f32[16,16,768]{2,1,0:T(8,128)S(1)}, f32[16,16,768]{2,1,0:T(8,128)}, u32[]{:S(2)}) copy-start(f32[16,16,768]{2,1,0:T(8,128)} %get-tuple-element.41) | copy-start | bytes 2359300
  49.4 1.7 %copy-start.3 = (f32[16,16,768]{2,1,0:T(8,128)S(1)}, f32[16,16,768]{2,1,0:T(8,128)}, u32[]{:S(2)}) copy-start(f32[16,16,768]{2,1,0:T(8,128)} %get-tuple-element.42) | copy-start | bytes 2359300
  49.4 1.9 %copy-start.5 = (f32[16,16,768]{2,1,0:T(8,128)S(1)}, f32[16,16,768]{2,1,0:T(8,128)}, u32[]{:S(2)}) copy-start(f32[16,16,768]{2,1,0:T(8,128)} %broadcast_in_dim.36) | copy-start | bytes 2359300
  49.4 2.1 %copy-start.7 = (f32[16,16,768]{2,1,0:T(8,128)S(1)}, f32[16,16,768]{2,1,0:T(8,128)}, u32[]{:S(2)}) copy-start(f32[16,16,768]{2,1,0:T(8,128)} %broadcast_in_dim.38) | copy-start | bytes 2359300
  49.4 2.4 %copy-start.9 = (f32[16,16,768]{2,1,0:T(8,128)S(1)}, f32[16,16,768]{2,1,0:T(8,128)}, u32[]{:S(2)}) copy-start(f32[16,16,768]{2,1,0:T(8,128)} %broadcast_in_dim.40) | copy-start | bytes 2359300
  49.4 2.6 %copy-start.11 = (f32[16,16,768]{2,1,0:T(8,128)S(1)}, f32[16,16,768]{2,1,0:T(8,128)}, u32[]{:S(2)}) copy-start(f32[16,16,768]{2,1,0:T(8,128)} %broadcast_in_dim.42) | copy-start | bytes 2359300
  49.7 10.4 %slice-start = ((s8[6291456]{0:T(1024)(128)(4,1)}), s8[4194304]{0:T(1024)(128)(4,1)S(1)}, s32[]{:S(2)}) async-start(s8[6291456]{0:T(1024)(128)(4,1)} %bitcast.305), calls=%async_computation | async-start | bytes 8388608
  52.0 8.0 %slice-start.1 = ((s8[6291456]{0:T(1024)(128)(4,1)}), s8[2097152]{0:T(1024)(128)(4,1)S(1)}, s32[]{:S(2)}) async-start(s8[6291456]{0:T(1024)(128)(4,1)} %bitcast.305), calls=%async_computation.1 | async-start | bytes 4194304
  71.3 0.9 copy-start.17
  71.3 1.4 %copy-start.15 = (f32[16,16,768]{2,1,0:T(8,128)S(1)}, f32[16,16,768]{2,1,0:T(8,128)}, u32[]{:S(2)}) copy-start(f32[16,16,768]{2,1,0:T(8,128)} %get-tuple-element.37) | copy-start | bytes 2359300
  72.2 1.0 copy-start.18
  72.7 1.1 %slice-start.2 = ((f32[16,16,768]{2,1,0:T(8,128)}), f32[15,16,768]{2,1,0:T(8,128)S(1)}, s32[]{:S(2)}) async-start(f32[16,16,768]{2,1,0:T(8,128)} %copy-done.16), calls=%async_computation.2 | async-start | bytes 1474560 | tf_op jit(solution)/shard_map/slice | solution.py:132
  72.7 1.3 %slice-start.3 = ((f32[16,16,768]{2,1,0:T(8,128)}), f32[15,16,768]{2,1,0:T(8,128)S(1)}, s32[]{:S(2)}) async-start(f32[16,16,768]{2,1,0:T(8,128)} %copy-done.17), calls=%async_computation.3 | async-start | bytes 1474560 | tf_op jit(solution)/shard_map/slice | solution.py:132
  73.2 3.8 %copy-start.19 = (f32[16,16,768]{2,1,0:T(8,128)}, f32[16,16,768]{2,1,0:T(8,128)S(1)}, u32[]{:S(2)}) copy-start(f32[16,16,768]{2,1,0:T(8,128)S(1)} %fusion.94) | copy-start | bytes 2359300
  77.0 4.8 %slice-start.4 = ((f32[16,16,768]{2,1,0:T(8,128)}), f32[1,16,768]{2,1,0:T(8,128)S(1)}, s32[]{:S(2)}) async-start(f32[16,16,768]{2,1,0:T(8,128)} %copy-done.17), calls=%async_computation.4 | async-start | bytes 98304 | tf_op jit(solution)/shard_map/slice | solution.py:135
  78.5 21.9 %collective-permute-start.8 = (f32[2,3,16,2,192]{4,3,2,1,0:T(2,128)S(1)}, f32[2,3,16,2,192]{4,3,2,1,0:T(2,128)S(1)}, u32[]{:S(2)}, u32[]{:S(2)}) collective-permute-start(f32[2,3,16,2,192]{4,3,2,1,0:T(2,128)S(1)} %bitcast.312), channel_id=1, source_target_pairs={{0,8},{8,0},{16,24},{24,16},{1,9},{9,1},{17,25},{25,17},{2,10},{10... | collective-permute-start | bytes 442376 | tf_op jit(solution)/shard_map/ppermute | solution.py:23
  81.9 3.6 %slice-start.5 = ((f32[16,16,768]{2,1,0:T(8,128)}), f32[1,16,768]{2,1,0:T(8,128)S(1)}, s32[]{:S(2)}) async-start(f32[16,16,768]{2,1,0:T(8,128)} %copy-done.18), calls=%async_computation.5 | async-start | bytes 98304 | tf_op jit(solution)/shard_map/slice | solution.py:135
  81.9 3.7 %slice-start.6 = ((f32[16,16,768]{2,1,0:T(8,128)}), f32[1,16,768]{2,1,0:T(8,128)S(1)}, s32[]{:S(2)}) async-start(f32[16,16,768]{2,1,0:T(8,128)} %copy-done.19), calls=%async_computation.6 | async-start | bytes 98304 | tf_op jit(solution)/shard_map/slice | solution.py:135
  82.0 5.7 %collective-permute-start.9 = (f32[2,1,16,2,192]{4,1,3,2,0:T(1,128)S(1)}, f32[2,1,16,2,192]{4,1,3,2,0:T(1,128)S(1)}, u32[]{:S(2)}, u32[]{:S(2)}) collective-permute-start(f32[2,1,16,2,192]{4,1,3,2,0:T(1,128)S(1)} %fusion.121), channel_id=1, source_target_pairs={{0,8},{8,0},{16,24},{24,16},{1,9},{9,1},{17,25},{25,17},{2,10},{10... | collective-permute-start | bytes 147464 | tf_op jit(solution)/shard_map/ppermute | solution.py:23
  83.4 19.2 %collective-permute-start.12 = (f32[2,3,16,2,192]{4,3,2,1,0:T(2,128)S(1)}, f32[2,3,16,2,192]{4,3,2,1,0:T(2,128)S(1)}, u32[]{:S(2)}, u32[]{:S(2)}) collective-permute-start(f32[2,3,16,2,192]{4,3,2,1,0:T(2,128)S(1)} %select_bitcast_fusion), channel_id=1, source_target_pairs={{0,8},{8,0},{16,24},{24,16},{1,9},{9,1},{17,25},{25,17},{2,10},{10... | collective-permute-start | bytes 442376 | tf_op jit(solution)/shard_map/ppermute | solution.py:23
  85.9 7.4 %collective-permute-start.13 = (f32[2,1,16,2,192]{4,1,3,2,0:T(1,128)S(1)}, f32[2,1,16,2,192]{4,1,3,2,0:T(1,128)S(1)}, u32[]{:S(2)}, u32[]{:S(2)}) collective-permute-start(f32[2,1,16,2,192]{4,1,3,2,0:T(1,128)S(1)} %fusion.122), channel_id=1, source_target_pairs={{0,8},{8,0},{16,24},{24,16},{1,9},{9,1},{17,25},{25,17},{2,10},{10... | collective-permute-start | bytes 147464 | tf_op jit(solution)/shard_map/ppermute | solution.py:23
  87.9 10.3 %collective-permute-start.11 = (f32[2,1,16,1,192]{4,1,3,2,0:T(1,128)S(1)}, f32[2,1,16,1,192]{4,1,3,2,0:T(1,128)S(1)}, u32[]{:S(2)}, u32[]{:S(2)}) collective-permute-start(f32[2,1,16,1,192]{4,1,3,2,0:T(1,128)S(1)} %fusion.125), channel_id=1, source_target_pairs={{0,16},{8,24},{16,0},{24,8},{1,17},{9,25},{17,1},{25,9},{2,18},{10... | collective-permute-start | bytes 73736 | tf_op jit(solution)/shard_map/ppermute | solution.py:23
  93.6 6.6 %collective-permute-start.15 = (f32[2,1,16,1,192]{4,1,3,2,0:T(1,128)S(1)}, f32[2,1,16,1,192]{4,1,3,2,0:T(1,128)S(1)}, u32[]{:S(2)}, u32[]{:S(2)}) collective-permute-start(f32[2,1,16,1,192]{4,1,3,2,0:T(1,128)S(1)} %fusion.126), channel_id=1, source_target_pairs={{0,16},{8,24},{16,0},{24,8},{1,17},{9,25},{17,1},{25,9},{2,18},{10... | collective-permute-start | bytes 73736 | tf_op jit(solution)/shard_map/ppermute | solution.py:23
  100.7 5.4 %collective-permute-start.10 = (f32[2,3,16,1,192]{4,3,2,1,0:T(1,128)S(1)}, f32[2,3,16,1,192]{4,3,2,1,0:T(1,128)S(1)}, u32[]{:S(2)}, u32[]{:S(2)}) collective-permute-start(f32[2,3,16,1,192]{4,3,2,1,0:T(1,128)S(1)} %fusion.120), channel_id=1, source_target_pairs={{0,16},{8,24},{16,0},{24,8},{1,17},{9,25},{17,1},{25,9},{2,18},{10... | collective-permute-start | bytes 221192 | tf_op jit(solution)/shard_map/ppermute | solution.py:23
  103.1 4.7 %collective-permute-start.14 = (f32[2,3,16,1,192]{4,3,2,1,0:T(1,128)S(1)}, f32[2,3,16,1,192]{4,3,2,1,0:T(1,128)S(1)}, u32[]{:S(2)}, u32[]{:S(2)}) collective-permute-start(f32[2,3,16,1,192]{4,3,2,1,0:T(1,128)S(1)} %fusion.119), channel_id=1, source_target_pairs={{0,16},{8,24},{16,0},{24,8},{1,17},{9,25},{17,1},{25,9},{2,18},{10... | collective-permute-start | bytes 221192 | tf_op jit(solution)/shard_map/ppermute | solution.py:23
where the time goes:
time: 109 us
  starting transfers between devices  39.1 us (36%)
  other arithmetic  38.5 us (35%)
  local copies, waits for them, and re-layouts  16.9 us (16%)
  waiting for transfers between devices  12.4 us (11%)
  between operations  1.65 us (2%)
    ppermute x4, starting transfers between devices, padded_2(): before = lax.ppermute(last, axis, up)  17.2 us
    unnamed x8, other arithmetic  16.7 us
    ppermute x8, starting transfers between devices, swapped(): lax.ppermute(x, axis, [(i, i ^ 1 << bit) for i in range(lax.axis_size(axi...  16.7 us
    ppermute x8, waiting for transfers between devices, swapped(): lax.ppermute(x, axis, [(i, i ^ 1 << bit) for i in range(lax.axis_size(axi...  8.8 us
    mul x2, other arithmetic, per_device(): rimmed = padded_2(voltage * tissue_float, (('depth', 0), ('area', 1)), 1)  8.35 us
    broadcast_in_dim x14, local copies, waits for them, and re-layouts, spread_blocks(): wide = jnp.broadcast_to(along, (fields, first, BLK, second, BLK, columns))  8.3 us
    ppermute x4, starting transfers between devices, padded_2(): after = lax.ppermute(leading, axis, down)  5.17 us
    unnamed x60, local copies, waits for them, and re-layouts  4.87 us
  transfers between devices with their start and end apart: 16, of which 9 were waited for; matrix products, arithmetic and copies ran while one was open for 11% of the time, Pallas kernels for 0%

commit v1 on v0

v1 whole, which is shorter than its diff:
```python
import functools
import math

import jax
import jax.numpy as jnp
from jax import lax
from jax.experimental import pallas as pl
from jax.experimental.pallas import tpu as pltpu
from jax.sharding import PartitionSpec as P

BLK = 4
CLASSES = 8
STEPS = 2
TIME_STEP = 0.15
SIGMA_LONG = 1.0
SIGMA_CROSS = 0.3
SLOPES = (8.0, -8.0, 6.0, 5.0, -5.0, -3.0)
MIDDLES = (0.2, 0.4, 0.3, 0.5, 0.6, 0.5)
RATES = (3.0, 0.5, 1.0, 0.8, 0.3, 0.1)
OPACITY = (0.012, 0.01)
TRACE = 3.0 * SIGMA_CROSS + (SIGMA_LONG - SIGMA_CROSS)
PLANES = 2
MESH = pl.DeviceIdType.MESH


def block_fields(tissue, fiber):
    kind = fiber.astype(jnp.float32)
    polar = math.pi * (kind + 0.5) / CLASSES
    azimuth = 2.3 * kind
    along_x = jnp.cos(polar)
    along_y = jnp.sin(polar) * jnp.cos(azimuth)
    along_z = jnp.sin(polar) * jnp.sin(azimuth)
    spread = SIGMA_LONG - SIGMA_CROSS
    parts = jnp.stack([
        tissue.astype(jnp.float32),
        TIME_STEP * (SIGMA_CROSS + spread * along_x * along_x),
        TIME_STEP * (SIGMA_CROSS + spread * along_y * along_y),
        TIME_STEP * (SIGMA_CROSS + spread * along_z * along_z),
        0.5 * TIME_STEP * spread * along_x * along_y,
        0.5 * TIME_STEP * spread * along_x * along_z,
        0.5 * TIME_STEP * spread * along_y * along_z,
    ])
    fields, first, second, third = parts.shape
    columns = third * BLK
    onehot = (jnp.arange(columns)[None, :] // BLK == jnp.arange(third)[:, None]).astype(jnp.float32)
    rows = jnp.repeat(parts, BLK, axis=2).reshape(fields * first * second * BLK, third)
    wide = jnp.dot(rows, onehot, precision=lax.Precision.HIGHEST, preferred_element_type=jnp.float32)
    return wide.reshape(fields, first, second * BLK, columns)


def halo_kernel(v_ref, mask_ref, hx_ref, hy_ref, xface, yface, xland, yland, send, recv):
    nx, ny = v_ref.shape[1], v_ref.shape[2]
    d, a = lax.axis_index("depth"), lax.axis_index("area")
    nd, na = lax.axis_size("depth"), lax.axis_size("area")
    links = [(i, j) for i in (-1, 0, 1) for j in (-1, 0, 1) if (i, j) != (0, 0)]

    def there(i, j):
        ok = jnp.bool_(True)
        if i:
            ok = jnp.logical_and(ok, d > 0 if i < 0 else d < nd - 1)
        if j:
            ok = jnp.logical_and(ok, a > 0 if j < 0 else a < na - 1)
        return ok

    xland[...] = jnp.zeros_like(xland)
    yland[...] = jnp.zeros_like(yland)
    barrier = pltpu.get_barrier_semaphore()
    for i, j in links:
        @pl.when(there(i, j))
        def _():
            pl.semaphore_signal(barrier, inc=1, device_id=(d + i, a + j), device_id_type=MESH)

    xface[0] = v_ref[0, 0] * mask_ref[0, 0]
    xface[1] = v_ref[0, nx - 1] * mask_ref[0, nx // BLK - 1]
    for x in range(nx):
        yface[0, x:x + 1] = v_ref[0, x, 0:1] * mask_ref[0, x // BLK, 0:1]
        yface[1, x:x + 1] = v_ref[0, x, ny - 1:ny] * mask_ref[0, x // BLK, ny - 1:ny]

    dn = (d > 0).astype(jnp.int32) + (d < nd - 1).astype(jnp.int32)
    an = (a > 0).astype(jnp.int32) + (a < na - 1).astype(jnp.int32)
    pl.semaphore_wait(barrier, dn + an + dn * an)

    def copy(n, i, j):
        if j == 0:
            src, dst = xface.at[0 if i < 0 else 1], xland.at[1 if i < 0 else 0]
        elif i == 0:
            src, dst = yface.at[0 if j < 0 else 1], yland.at[1 if j < 0 else 0, pl.ds(0, nx)]
        else:
            src = yface.at[0 if j < 0 else 1, pl.ds(0 if i < 0 else nx - 1, 1)]
            dst = yland.at[1 if j < 0 else 0, pl.ds(nx + 8 if i < 0 else nx, 1)]
        back = links.index((-i, -j))
        return pltpu.make_async_remote_copy(
            src_ref=src, dst_ref=dst, send_sem=send.at[n], recv_sem=recv.at[back],
            device_id=(d + i, a + j), device_id_type=MESH)

    def arrival(n, i, j):
        back = links.index((-i, -j))
        if j == 0:
            src, dst = xface.at[0 if i > 0 else 1], xland.at[0 if i < 0 else 1]
        elif i == 0:
            src, dst = yface.at[0 if j > 0 else 1], yland.at[0 if j < 0 else 1, pl.ds(0, nx)]
        else:
            src = yface.at[0 if j > 0 else 1, pl.ds(0 if i > 0 else nx - 1, 1)]
            dst = yland.at[0 if j < 0 else 1, pl.ds(nx if i < 0 else nx + 8, 1)]
        return pltpu.make_async_remote_copy(
            src_ref=src, dst_ref=dst, send_sem=send.at[back], recv_sem=recv.at[n],
            device_id=(d + i, a + j), device_id_type=MESH)

    for n, (i, j) in enumerate(links):
        @pl.when(there(i, j))
        def _():
            copy(n, i, j).start()
    for n, (i, j) in enumerate(links):
        @pl.when(there(i, j))
        def _():
            copy(n, i, j).wait_send()
            arrival(n, i, j).wait_recv()
    hx_ref[...] = xland[...]
    hy_ref[...] = yland[...]


def halos(states, mask, collective):
    _, nx, ny, nz = states.shape
    whole = pl.BlockSpec(memory_space=pltpu.VMEM)
    return pl.pallas_call(
        halo_kernel,
        grid=(1,),
        out_shape=(jax.ShapeDtypeStruct((2, ny, nz), jnp.float32),
                   jax.ShapeDtypeStruct((2, nx + 16, nz), jnp.float32)),
        in_specs=[pl.BlockSpec((1, nx, ny, nz), lambda i: (0, 0, 0, 0)),
                  pl.BlockSpec((1,) + mask.shape[1:], lambda i: (0, 0, 0, 0))],
        out_specs=(whole, whole),
        scratch_shapes=[
            pltpu.VMEM((2, ny, nz), jnp.float32),
            pltpu.VMEM((2, nx, nz), jnp.float32),
            pltpu.VMEM((2, ny, nz), jnp.float32),
            pltpu.VMEM((2, nx + 16, nz), jnp.float32),
            pltpu.SemaphoreType.DMA((8,)),
            pltpu.SemaphoreType.DMA((8,)),
        ],
        compiler_params=pltpu.CompilerParams(
            collective_id=collective, has_side_effects=True, vmem_limit_bytes=16 << 20),
        name="halo%d" % collective,
    )(states, mask)


def step_kernel(in_ref, v_ref, field_ref, hx_ref, hy_ref, out_ref, acc_ref, pad):
    nx, ny, nz = v_ref.shape[1:]
    i = pl.program_id(0)

    @pl.when(i == 0)
    def _():
        pad[:, :, nz:] = jnp.zeros((nx + 2, ny + 16, pad.shape[2] - nz), jnp.float32)
        acc_ref[...] = jnp.zeros_like(acc_ref)
        for x in range(nx):
            pad[x + 1, 8:8 + ny, :nz] = v_ref[0, x] * field_ref[0, x // BLK]
        pad[0, 8:8 + ny, :nz] = hx_ref[0]
        pad[nx + 1, 8:8 + ny, :nz] = hx_ref[1]
        for side, row in ((0, 7), (1, 8 + ny)):
            pad[0, row:row + 1, :nz] = hy_ref[side, nx:nx + 1]
            pad[nx + 1, row:row + 1, :nz] = hy_ref[side, nx + 8:nx + 9]
            for x in range(nx):
                pad[x + 1, row:row + 1, :nz] = hy_ref[side, x:x + 1]

    wide = pad.shape[2]

    def plane(p):
        x = i * PLANES + p
        block = x // BLK
        for top in range(0, ny, 8):
            def rows(dx, dy):
                return pad[x + 1 + dx, 8 + top + dy:16 + top + dy, :]

            centre = rows(0, 0)
            up, down = rows(0, -1), rows(0, 1)
            after, before = rows(1, 0), rows(-1, 0)
            slope_x = after - before
            slope_y = down - up
            slope_xy = (rows(1, 1) - rows(-1, 1)) - (rows(1, -1) - rows(-1, -1))

            def ahead(item):
                return pltpu.roll(item, wide - 1, 1)

            def behind(item):
                return pltpu.roll(item, 1, 1)

            second_z = ahead(centre) + behind(centre)
            slope_xz = ahead(slope_x) - behind(slope_x)
            slope_yz = ahead(slope_y) - behind(slope_y)
            second_x = after + before
            second_y = up + down
            for left in range(0, nz, 128):
                zs = slice(left, left + 128)
                at = (slice(top, top + 8), zs)

                def comp(k):
                    return field_ref[k, block, top:top + 8, zs]

                w = ((1.0 - 2.0 * TIME_STEP * TRACE) * centre[:, zs]
                     + comp(1) * second_x[:, zs] + comp(2) * second_y[:, zs] + comp(3) * second_z[:, zs]
                     + comp(4) * slope_xy[:, zs] + comp(5) * slope_xz[:, zs] + comp(6) * slope_yz[:, zs])
                mask = comp(0)
                tissue = mask > 0.5
                h = []
                for k in range(6):
                    decay = math.exp(-TIME_STEP * RATES[k])
                    half = 0.5 * (1.0 - decay)
                    old = in_ref[k + 1, p, top:top + 8, zs]
                    gate = old * decay + (half + half * jnp.tanh(
                        (0.5 * SLOPES[k]) * w - 0.5 * SLOPES[k] * MIDDLES[k]))
                    h.append(gate)
                    out_ref[k + 1, p, top:top + 8, zs] = jnp.where(tissue, gate, old)
                pair = h[3] * h[4]
                current = (
                    (h[0] * h[0]) * (h[0] * h[1]) * (2.0 * w - 2.4)
                    + h[2] * h[2] * (w + 0.1)
                    + pair * (0.6 * w - 0.54)
                    + (1.0 + h[5]) * (0.2 * w - 0.01)
                )
                old_v = in_ref[0, p, top:top + 8, zs]
                old_ca = in_ref[7, p, top:top + 8, zs]
                volt = jnp.where(tissue, w - TIME_STEP * current, old_v)
                calc = jnp.where(
                    tissue,
                    (1.0 - 0.8 * TIME_STEP) * old_ca + (1.5 * TIME_STEP) * pair * (1.0 - old_ca),
                    old_ca)
                out_ref[0, p, top:top + 8, zs] = volt
                out_ref[7, p, top:top + 8, zs] = calc
                for which, q in enumerate((volt, calc)):
                    half = (0.5 * OPACITY[which]) * mask
                    alpha = half + half * jnp.tanh(3.0 * q - 1.2)
                    total = acc_ref[(3 * which,) + at]
                    weight = (1.0 - total) * alpha
                    acc_ref[(3 * which,) + at] = total + weight
                    acc_ref[(3 * which + 1,) + at] += weight * jnp.tanh(2.5 * q - 1.25)
                    off = q - 0.5
                    acc_ref[(3 * which + 2,) + at] += weight * jnp.exp(-6.0 * off * off)

    for p in range(PLANES):
        plane(p)


def advance(states, fields, hx, hy):
    _, nx, ny, nz = states.shape
    whole = pl.BlockSpec(memory_space=pltpu.VMEM)
    return pl.pallas_call(
        step_kernel,
        grid=(nx // PLANES,),
        out_shape=(jax.ShapeDtypeStruct(states.shape, jnp.float32),
                   jax.ShapeDtypeStruct((6, ny, nz), jnp.float32)),
        in_specs=[pl.BlockSpec((8, PLANES, ny, nz), lambda i: (0, i, 0, 0)),
                  pl.BlockSpec((1, nx, ny, nz), lambda i: (0, 0, 0, 0)),
                  whole, whole, whole],
        out_specs=(pl.BlockSpec((8, PLANES, ny, nz), lambda i: (0, i, 0, 0)),
                   pl.BlockSpec((6, ny, nz), lambda i: (0, 0, 0))),
        scratch_shapes=[pltpu.VMEM((nx + 2, ny + 16, nz + 128), jnp.float32)],
        compiler_params=pltpu.CompilerParams(vmem_limit_bytes=32 << 20),
        name="step",
    )(states, states, fields, hx, hy)


def blend_kernel(part_ref, out_ref, land, send, recv):
    count = part_ref.shape[0]
    me = lax.axis_index("depth")
    barrier = pltpu.get_barrier_semaphore()
    for k in range(1, count):
        pl.semaphore_signal(barrier, inc=1, device_id={"depth": lax.rem(me + k, count)}, device_id_type=MESH)
    pl.semaphore_wait(barrier, count - 1)
    copies = []
    for k in range(1, count):
        to = lax.rem(me + k, count)
        copy = pltpu.make_async_remote_copy(
            src_ref=part_ref.at[to], dst_ref=land.at[k], send_sem=send.at[k], recv_sem=recv.at[k],
            device_id={"depth": to}, device_id_type=MESH)
        copy.start()
        copies.append(copy)
    land[0] = part_ref[me]
    for copy in copies:
        copy.wait()
    images, ny = out_ref.shape[0], out_ref.shape[2]
    for n in range(images):
        def at(group, channel):
            start = (3 * n + channel) * ny
            return land[lax.rem(me - group + count, count), start:start + ny]

        total, warm, green = at(0, 0), at(0, 1), at(0, 2)
        for group in range(1, count):
            through = 1.0 - total
            warm = warm + through * at(group, 1)
            green = green + through * at(group, 2)
            total = total + through * at(group, 0)
        out_ref[n, 0] = 0.5 * (total + warm)
        out_ref[n, 1] = green
        out_ref[n, 2] = 0.5 * (total - warm)
        out_ref[n, 3] = total


def blend(parts):
    steps, _, ny, nz = parts.shape
    count = lax.axis_size("depth")
    width = nz // count
    split = jnp.moveaxis(parts.reshape(steps * 6 * ny, count, width), 1, 0)
    out = pl.pallas_call(
        blend_kernel,
        out_shape=jax.ShapeDtypeStruct((steps * 2, 4, ny, width), jnp.float32),
        in_specs=[pl.BlockSpec(memory_space=pltpu.VMEM)],
        out_specs=pl.BlockSpec(memory_space=pltpu.VMEM),
        scratch_shapes=[
            pltpu.VMEM((count, steps * 6 * ny, width), jnp.float32),
            pltpu.SemaphoreType.DMA((count,)),
            pltpu.SemaphoreType.DMA((count,)),
        ],
        compiler_params=pltpu.CompilerParams(
            collective_id=7, has_side_effects=True, vmem_limit_bytes=16 << 20),
        name="blend",
    )(split)
    return out.reshape(steps, 2, 4, ny, width)


def per_device(states, tissue, fiber):
    fields = block_fields(tissue, fiber)
    parts = []
    for step in range(STEPS):
        hx, hy = halos(states, fields, step)
        states, part = advance(states, fields, hx, hy)
        parts.append(part)
    return states, blend(jnp.stack(parts))


def solution(mesh):
    return jax.shard_map(
        per_device,
        mesh=mesh,
        in_specs=(
            P(None, "depth", "area", None),
            P("depth", "area", None),
            P("depth", "area", None),
        ),
        out_specs=(P(None, "depth", "area", None), P(None, None, None, "area", "depth")),
        check_vma=False,
    )
```

time: 109 us -> 53.3 us (0.49)
  Pallas kernels: 0 us -> 40.1 us
  starting transfers between devices: 39.1 us -> 0 us
  other arithmetic: 38.5 us -> 6.47 us
  waiting for transfers between devices: 12.4 us -> 0 us
  local copies, waits for them, and re-layouts: 16.9 us -> 4.5 us
    pallas_call x0 -> x5, Pallas kernels: none -> 40.1 us  [the longest x1 13.7 us: blend(): pl.pallas_call(blend_kernel, out_shape=jax.ShapeDtypeStruct((steps * 2, 4...]
    ppermute x16 -> x0, starting transfers between devices: 39.1 us -> none  [the longest x4 17.2 us: padded_2(): before = lax.ppermute(last, axis, up)]
    ppermute x16 -> x0, waiting for transfers between devices: 12.4 us -> none  [the longest x8 8.8 us: swapped(): lax.ppermute(x, axis, [(i, i ^ 1 << bit) for i in range(lax.axis_size(axi...]
    unnamed x8 -> x6, other arithmetic: 16.7 us -> 5.45 us
    mul x3 -> x0, other arithmetic: 9.33 us -> none  [the longest x2 8.35 us: per_device(): rimmed = padded_2(voltage * tissue_float, (('depth', 0), ('area', 1)), 1)]
    broadcast_in_dim x14 -> x1, local copies, waits for them, and re-layouts: 8.3 us -> 0.11 us  [block_fields(): jnp.repeat(parts, BLK, axis=2).reshape(fields * first * second * BLK, third)]
    another operation x11 -> x2, other arithmetic: 4.68 us -> 1.01 us  [the longest x1 0.97 us: block_fields(): jnp.stack([tissue.astype(jnp.float32), TIME_STEP * (SIGMA_CROSS + spread...]
    reduce_sum x1 -> x0, other arithmetic: 2.93 us -> none  [march(): colour = jnp.stack([jnp.sum(weight * item, axis=0) for item in colours])]
  transfers between devices with their start and end apart: 16 -> 0, of which waited for: 9 -> 0; matrix products, arithmetic and copies ran while one was open for 11% -> 0% of each run, Pallas kernels for 0% -> 0%
where the time goes in v1:
time: 53.3 us; the launch traced here: 52.5 us
  Pallas kernels  40.1 us (75%)
  other arithmetic  6.47 us (12%)
  local copies, waits for them, and re-layouts  4.5 us (8%)
  matrix products  0.78 us (1%)
  between operations  0.73 us (1%)
    pallas_call x1, Pallas kernels, blend(): pl.pallas_call(blend_kernel, out_shape=jax.ShapeDtypeStruct((steps * 2, 4...  13.7 us
    pallas_call x2, Pallas kernels, halos(): pl.pallas_call(halo_kernel, grid=(1,), out_shape=(jax.ShapeDtypeStruct((2...  13.3 us
    pallas_call x2, Pallas kernels, advance(): pl.pallas_call(step_kernel, grid=(nx // PLANES,), out_shape=(jax.ShapeDty...  13.1 us
    unnamed x6, other arithmetic  5.45 us
    unnamed x5, local copies, waits for them, and re-layouts  3.49 us

profile of v1, /device:TPU:0, one launch (start us, length us, event | category | flops | bytes accessed | tf_op | source)
XLA Modules:
  0.0 52.5 jit_solution(2608281309879704674)
XLA Ops:
  0.6 0.7 %constant_dynamic-update-slice_fusion.3 = f32[7,4,4,192]{3,2,1,0:T(4,128)S(1)} fusion(s32[4,4,192]{2,1,0:T(4,128)} %param.4), kind=kLoop, calls=%fused_computation.24 | loop fusion | flops 3071 | bytes 28672
  1.4 0.9 %fusion.7 = f32[7,4,4,192]{3,2,1,0:T(4,128)S(1)} fusion(f32[7,4,4,192]{3,2,1,0:T(4,128)S(1)} %constant_dynamic-update-slice_fusion.3, s32[4,4,192]{2,1,0:T(4,128)} %param.5), kind=kLoop, calls=%fused_computation.12 | loop fusion | flops 21504 | bytes 28672
  2.2 1.0 %fusion.11 = f32[7,4,4,192]{3,2,1,0:T(4,128)S(1)} fusion(f32[7,4,4,192]{3,2,1,0:T(4,128)S(1)} %fusion.7, s32[4,4,192]{2,1,0:T(4,128)} %param.5), kind=kLoop, calls=%fused_computation.16 | loop fusion | flops 27648 | bytes 28672
  3.2 1.0 %fusion.15 = f32[7,4,4,192]{3,2,1,0:T(4,128)S(1)} fusion(f32[7,4,4,192]{3,2,1,0:T(4,128)S(1)} %fusion.11, s32[4,4,192]{2,1,0:T(4,128)} %param.5), kind=kLoop, calls=%fused_computation.20 | loop fusion | flops 27648 | bytes 28672
  4.2 1.0 %constant_dynamic-update-slice_fusion.2 = f32[7,4,4,192]{3,2,1,0:T(4,128)S(1)} fusion(f32[7,4,4,192]{3,2,1,0:T(4,128)S(1)} %fusion.15, s32[4,4,192]{2,1,0:T(4,128)} %param.5), kind=kLoop, calls=%fused_computation.23 | loop fusion | flops 21504 | bytes 28672
  5.1 1.0 %constant_dynamic-update-slice_fusion.1 = f32[7,4,4,192]{3,2,1,0:T(4,128)S(1)} fusion(f32[7,4,4,192]{3,2,1,0:T(4,128)S(1)} %constant_dynamic-update-slice_fusion.2, s32[4,4,192]{2,1,0:T(4,128)} %param.5), kind=kLoop, calls=%fused_computation.22 | loop fusion | flops 21504 | bytes 28672
  6.1 1.0 %constant_dynamic-update-slice_fusion = f32[7,4,4,192]{3,2,1,0:T(4,128)S(1)} fusion(f32[7,4,4,192]{3,2,1,0:T(4,128)S(1)} %constant_dynamic-update-slice_fusion.1, s32[4,4,192]{2,1,0:T(4,128)} %param.5), kind=kLoop, calls=%fused_computation.21 | loop fusion | flops 24576 | bytes 28672 | tf_op jit(solution)/shard_map/stack | solution.py:34
  7.1 0.1 broadcast_in_dim.2
  7.2 0.2 dot_general.5
  7.4 0.8 %fusion.1.mask_ref.field_ref = f32[7,4,16,768]{3,2,1,0:T(8,128)S(1)} fusion(f32[7,4,16,192]{3,2,1,0:T(8,128)S(1)} %dot_general.5, s32[768]{0:T(1024)S(1)} %add_select_fusion), kind=kOutput, calls=%fused_computation.4 | convolution fusion | flops 792870912 | bytes 1723392 | tf_op jit(solution)/shard_map/dot_general | solution.py:47
  8.1 0.0 copy-start
  8.2 2.8 %copy-done = f32[8,16,16,768]{3,2,1,0:T(8,128)S(1)} copy-done((f32[8,16,16,768]{3,2,1,0:T(8,128)S(1)}, f32[8,16,16,768]{3,2,1,0:T(8,128)}, u32[]{:S(2)}) %copy-start) | copy-done | bytes 6291480
  10.9 0.0 copy-start.1
  10.9 6.8 %halo0.1 = (f32[2,16,768]{2,1,0:T(8,128)S(1)}, f32[2,32,768]{2,1,0:T(8,128)S(1)}) custom-call(f32[8,16,16,768]{3,2,1,0:T(8,128)S(1)} %copy-done, f32[7,4,16,768]{3,2,1,0:T(8,128)S(1)} %fusion.1.mask_ref.field_ref), custom_call_target="tpu_custom_call" | custom-call | tf_op jit(solution)/shard_map/halo0/pallas_call | solution.py:125
  17.8 0.0 copy-done.1
  17.8 6.0 %step.2 = (f32[8,16,16,768]{3,2,1,0:T(8,128)S(1)}, f32[6,16,768]{2,1,0:T(8,128)S(1)}) custom-call(f32[8,16,16,768]{3,2,1,0:T(8,128)S(1)} %copy-done.1, f32[8,16,16,768]{3,2,1,0:T(8,128)S(1)} %copy-done.1, f32[7,4,16,768]{3,2,1,0:T(8,128)S(1)} %fusion.1.mask_ref.field_ref, f32[2,16,768]{2,1,0:T(8,128)S(1)} %get-tuple-element.10.hx_ref, ...), custom_call_target="tpu_custom_call" | custom-call | tf_op jit(solution)/shard_map/step/pallas_call | solution.py:246
  23.8 6.4 %halo1.1 = (f32[2,16,768]{2,1,0:T(8,128)S(1)}, f32[2,32,768]{2,1,0:T(8,128)S(1)}) custom-call(f32[8,16,16,768]{3,2,1,0:T(8,128)S(1)} %get-tuple-element.12.v_ref.in_ref, f32[7,4,16,768]{3,2,1,0:T(8,128)S(1)} %fusion.1.mask_ref.field_ref), custom_call_target="tpu_custom_call" | custom-call | tf_op jit(solution)/shard_map/halo1/pallas_call | solution.py:125
  30.2 7.1 %step.3 = (f32[8,16,16,768]{3,2,1,0:T(8,128)}, f32[6,16,768]{2,1,0:T(8,128)S(1)}) custom-call(f32[8,16,16,768]{3,2,1,0:T(8,128)S(1)} %get-tuple-element.12.v_ref.in_ref, f32[8,16,16,768]{3,2,1,0:T(8,128)S(1)} %get-tuple-element.12.v_ref.in_ref, f32[7,4,16,768]{3,2,1,0:T(8,128)S(1)} %fusion.1.mask_ref.field_ref, f32[2,16,768]{2,1,0:T(8,128)S(1)} %get-tuple-element.13.hx_ref, ...), custom_call_target="tpu_custom_call" | custom-call | tf_op jit(solution)/shard_map/step/pallas_call | solution.py:246
  37.4 0.6 %reshape.50 = f32[192,4,192]{2,1,0:T(4,128)S(1)} reshape(f32[2,6,16,768]{3,2,1,0:T(8,128)S(1)} %pad_maximum_fusion) | data formatting | bytes 1179648 | tf_op jit(solution)/shard_map/reshape | solution.py:302
  38.0 0.2 copy.8
  38.1 13.7 %blend.1 = f32[4,4,16,192]{3,2,1,0:T(8,128)S(1)} custom-call(f32[4,192,192]{2,1,0:T(8,128)S(1)} %bitcast.34), custom_call_target="tpu_custom_call" | custom-call | tf_op jit(solution)/shard_map/blend/pallas_call | solution.py:303
  51.8 0.7 %copy.16 = f32[2,2,4,16,192]{4,3,2,1,0:T(8,128)} copy(f32[2,2,4,16,192]{4,3,2,1,0:T(8,128)S(1)} %bitcast.35) | data formatting | bytes 393216
  (2 shorter events, 0.0 us)
Async XLA Ops:
  8.1 2.8 %copy-start = (f32[8,16,16,768]{3,2,1,0:T(8,128)S(1)}, f32[8,16,16,768]{3,2,1,0:T(8,128)}, u32[]{:S(2)}) copy-start(f32[8,16,16,768]{3,2,1,0:T(8,128)} %v_ref.3) | copy-start | bytes 18874372
  10.9 6.8 %copy-start.1 = (f32[8,16,16,768]{3,2,1,0:T(8,128)S(1)}, f32[8,16,16,768]{3,2,1,0:T(8,128)}, u32[]{:S(2)}) copy-start(f32[8,16,16,768]{3,2,1,0:T(8,128)} %v_ref.3) | copy-start | bytes 18874372

commit v2 on v1

--- a/solution.py
+++ b/solution.py
@@ -23,29 +23,56 @@
 MESH = pl.DeviceIdType.MESH
 
 
-def block_fields(tissue, fiber):
-    kind = fiber.astype(jnp.float32)
+def components(kind):
     polar = math.pi * (kind + 0.5) / CLASSES
     azimuth = 2.3 * kind
-    along_x = jnp.cos(polar)
-    along_y = jnp.sin(polar) * jnp.cos(azimuth)
-    along_z = jnp.sin(polar) * jnp.sin(azimuth)
+    fx = math.cos(polar)
+    fy = math.sin(polar) * math.cos(azimuth)
+    fz = math.sin(polar) * math.sin(azimuth)
     spread = SIGMA_LONG - SIGMA_CROSS
-    parts = jnp.stack([
-        tissue.astype(jnp.float32),
-        TIME_STEP * (SIGMA_CROSS + spread * along_x * along_x),
-        TIME_STEP * (SIGMA_CROSS + spread * along_y * along_y),
-        TIME_STEP * (SIGMA_CROSS + spread * along_z * along_z),
-        0.5 * TIME_STEP * spread * along_x * along_y,
-        0.5 * TIME_STEP * spread * along_x * along_z,
-        0.5 * TIME_STEP * spread * along_y * along_z,
-    ])
-    fields, first, second, third = parts.shape
+    return (
+        TIME_STEP * (SIGMA_CROSS + spread * fx * fx),
+        TIME_STEP * (SIGMA_CROSS + spread * fy * fy),
+        TIME_STEP * (SIGMA_CROSS + spread * fz * fz),
+        0.5 * TIME_STEP * spread * fx * fy,
+        0.5 * TIME_STEP * spread * fx * fz,
+        0.5 * TIME_STEP * spread * fy * fz,
+    )
+
+
+def fields_kernel(tissue_ref, fiber_ref, out_ref):
+    first, second, third = tissue_ref.shape
     columns = third * BLK
-    onehot = (jnp.arange(columns)[None, :] // BLK == jnp.arange(third)[:, None]).astype(jnp.float32)
-    rows = jnp.repeat(parts, BLK, axis=2).reshape(fields * first * second * BLK, third)
-    wide = jnp.dot(rows, onehot, precision=lax.Precision.HIGHEST, preferred_element_type=jnp.float32)
-    return wide.reshape(fields, first, second * BLK, columns)
+    table = [components(c) for c in range(CLASSES)]
+    onehot = (lax.broadcasted_iota(jnp.int32, (third, columns), 1) // BLK
+              == lax.broadcasted_iota(jnp.int32, (third, columns), 0)).astype(jnp.float32)
+    for x in range(first):
+        kind = fiber_ref[x]
+        parts = [tissue_ref[x].astype(jnp.float32)]
+        for k in range(6):
+            value = jnp.full(kind.shape, table[0][k], jnp.float32)
+            for c in range(1, CLASSES):
+                value = jnp.where(kind == c, table[c][k], value)
+            parts.append(value)
+        rows = jnp.concatenate(parts, axis=0)
+        wide = jnp.dot(rows, onehot, precision=lax.Precision.HIGHEST, preferred_element_type=jnp.float32)
+        for k in range(7):
+            for y in range(second):
+                row = k * second + y
+                out_ref[k, x, y * BLK:(y + 1) * BLK, :] = jnp.broadcast_to(wide[row:row + 1], (BLK, columns))
+
+
+def block_fields(tissue, fiber):
+    first, second, third = tissue.shape
+    whole = pl.BlockSpec(memory_space=pltpu.VMEM)
+    return pl.pallas_call(
+        fields_kernel,
+        out_shape=jax.ShapeDtypeStruct((7, first, second * BLK, third * BLK), jnp.float32),
+        in_specs=[whole, whole],
+        out_specs=whole,
+        compiler_params=pltpu.CompilerParams(vmem_limit_bytes=16 << 20),
+        name="fields",
+    )(tissue, fiber)
 
 
 def halo_kernel(v_ref, mask_ref, hx_ref, hy_ref, xface, yface, xland, yland, send, recv):
@@ -259,8 +286,11 @@
     )(states, states, fields, hx, hy)
 
 
-def blend_kernel(part_ref, out_ref, land, send, recv):
-    count = part_ref.shape[0]
+def blend_kernel(base, rem, *refs):
+    kinds = (base > 0) + (rem > 0)
+    parts, out_ref, lands = refs[:kinds], refs[kinds], refs[kinds + 1:2 * kinds + 1]
+    send, recv = refs[2 * kinds + 1:]
+    count = parts[0].shape[0]
     me = lax.axis_index("depth")
     barrier = pltpu.get_barrier_semaphore()
     for k in range(1, count):
@@ -269,51 +299,71 @@
     copies = []
     for k in range(1, count):
         to = lax.rem(me + k, count)
-        copy = pltpu.make_async_remote_copy(
-            src_ref=part_ref.at[to], dst_ref=land.at[k], send_sem=send.at[k], recv_sem=recv.at[k],
-            device_id={"depth": to}, device_id_type=MESH)
-        copy.start()
-        copies.append(copy)
-    land[0] = part_ref[me]
+        for n in range(kinds):
+            copy = pltpu.make_async_remote_copy(
+                src_ref=parts[n].at[to], dst_ref=lands[n].at[k], send_sem=send.at[n, k],
+                recv_sem=recv.at[n, k], device_id={"depth": to}, device_id_type=MESH)
+            copy.start()
+            copies.append(copy)
+    for n in range(kinds):
+        lands[n][0] = parts[n][me]
     for copy in copies:
         copy.wait()
     images, ny = out_ref.shape[0], out_ref.shape[2]
-    for n in range(images):
-        def at(group, channel):
-            start = (3 * n + channel) * ny
-            return land[lax.rem(me - group + count, count), start:start + ny]
-
-        total, warm, green = at(0, 0), at(0, 1), at(0, 2)
-        for group in range(1, count):
-            through = 1.0 - total
-            warm = warm + through * at(group, 1)
-            green = green + through * at(group, 2)
-            total = total + through * at(group, 0)
-        out_ref[n, 0] = 0.5 * (total + warm)
-        out_ref[n, 1] = green
-        out_ref[n, 2] = 0.5 * (total - warm)
-        out_ref[n, 3] = total
+    pieces = [(0, 0, base)] if base else []
+    if rem:
+        pieces.append((kinds - 1, base, rem))
+    for which, left, width in pieces:
+        height = lands[which].shape[1]
+        for n in range(images):
+            def at(group, channel):
+                start = (3 * n + channel) * ny
+                lane = (start // height) * width
+                start = start % height
+                return lands[which][lax.rem(me - group + count, count), start:start + ny, lane:lane + width]
+
+            total, warm, green = at(0, 0), at(0, 1), at(0, 2)
+            for group in range(1, count):
+                through = 1.0 - total
+                warm = warm + through * at(group, 1)
+                green = green + through * at(group, 2)
+                total = total + through * at(group, 0)
+            zs = slice(left, left + width)
+            out_ref[n, 0, :, zs] = 0.5 * (total + warm)
+            out_ref[n, 1, :, zs] = green
+            out_ref[n, 2, :, zs] = 0.5 * (total - warm)
+            out_ref[n, 3, :, zs] = total
 
 
 def blend(parts):
     steps, _, ny, nz = parts.shape
     count = lax.axis_size("depth")
     width = nz // count
-    split = jnp.moveaxis(parts.reshape(steps * 6 * ny, count, width), 1, 0)
+    rem = width % 128
+    base = width - rem
+    rows = steps * 6 * ny
+    split = jnp.moveaxis(parts.reshape(rows, count, width), 1, 0)
+    sent = [split[:, :, :base]] if base else []
+    if rem:
+        fold = 128 // rem
+        while (steps * 6) % fold:
+            fold -= 1
+        tall = rows // fold
+        sent.append(jnp.concatenate(
+            [split[:, f * tall:(f + 1) * tall, base:] for f in range(fold)], axis=2))
     out = pl.pallas_call(
-        blend_kernel,
+        functools.partial(blend_kernel, base, rem),
         out_shape=jax.ShapeDtypeStruct((steps * 2, 4, ny, width), jnp.float32),
-        in_specs=[pl.BlockSpec(memory_space=pltpu.VMEM)],
+        in_specs=[pl.BlockSpec(memory_space=pltpu.VMEM)] * len(sent),
         out_specs=pl.BlockSpec(memory_space=pltpu.VMEM),
-        scratch_shapes=[
-            pltpu.VMEM((count, steps * 6 * ny, width), jnp.float32),
-            pltpu.SemaphoreType.DMA((count,)),
-            pltpu.SemaphoreType.DMA((count,)),
+        scratch_shapes=[pltpu.VMEM(item.shape, jnp.float32) for item in sent] + [
+            pltpu.SemaphoreType.DMA((len(sent), count)),
+            pltpu.SemaphoreType.DMA((len(sent), count)),
         ],
         compiler_params=pltpu.CompilerParams(
             collective_id=7, has_side_effects=True, vmem_limit_bytes=16 << 20),
         name="blend",
-    )(split)
+    )(*sent)
     return out.reshape(steps, 2, 4, ny, width)
 
 
@@ -321,7 +371,7 @@
     fields = block_fields(tissue, fiber)
     parts = []
     for step in range(STEPS):
-        hx, hy = halos(states, fields, step)
+        hx, hy = halos(states if step else states[:1], fields, step)
         states, part = advance(states, fields, hx, hy)
         parts.append(part)
     return states, blend(jnp.stack(parts))

time: 53.3 us -> 47.3 us (0.89)
  other arithmetic: 6.47 us -> 0.16 us
  local copies, waits for them, and re-layouts: 4.5 us -> 6.9 us
  Pallas kernels: 40.1 us -> 39.1 us
  matrix products: 0.78 us -> 0 us
    unnamed x6 -> x0, other arithmetic: 5.45 us -> none
    unnamed x5 -> x7, local copies, waits for them, and re-layouts: 3.49 us -> 4.91 us
    slice x0 -> x3, local copies, waits for them, and re-layouts: none -> 1.24 us  [the longest x1 1.19 us: per_device(): hx, hy = halos(states if step else states[:1], fields, step)]
    another operation x1 -> x0, other arithmetic: 0.97 us -> none  [block_fields(): jnp.stack([tissue.astype(jnp.float32), TIME_STEP * (SIGMA_CROSS + spread...]
    pallas_call x1 -> x2, Pallas kernels: 13.7 us -> 12.8 us  [the longest x1 11.8 us: blend(): pl.pallas_call(functools.partial(blend_kernel, base, rem), out_shape=jax....]
    dot_general x1 -> x0, matrix products: 0.78 us -> none  [block_fields(): jnp.dot(rows, onehot, precision=lax.Precision.HIGHEST, preferred_element_...]
where the time goes in v2:
time: 47.3 us; the launch traced here: 46.9 us
  Pallas kernels  39.1 us (83%)
  local copies, waits for them, and re-layouts  6.9 us (15%)
  between operations  0.73 us (2%)
    pallas_call x2, Pallas kernels, halos(): pl.pallas_call(halo_kernel, grid=(1,), out_shape=(jax.ShapeDtypeStruct((2...  13.3 us
    pallas_call x2, Pallas kernels, advance(): pl.pallas_call(step_kernel, grid=(nx // PLANES,), out_shape=(jax.ShapeDty...  13.1 us
    pallas_call x1, Pallas kernels, blend(): pl.pallas_call(functools.partial(blend_kernel, base, rem), out_shape=jax....  11.8 us
    unnamed x7, local copies, waits for them, and re-layouts  4.91 us
    slice x1, local copies, waits for them, and re-layouts, per_device(): hx, hy = halos(states if step else states[:1], fields, step)  1.19 us
    pallas_call x1, Pallas kernels, block_fields(): pl.pallas_call(fields_kernel, out_shape=jax.ShapeDtypeStruct((7, first, s...  1.04 us

profile of v2, /device:TPU:0, one launch (start us, length us, event | category | flops | bytes accessed | tf_op | source)
XLA Modules:
  0.0 46.9 jit_solution(13869348058773017646)
XLA Ops:
  0.6 1.2 %slice.12.v_ref = f32[1,16,16,768]{3,2,1,0:T(8,128)S(1)} slice(f32[8,16,16,768]{3,2,1,0:T(8,128)} %v_ref.1), slice={[0:1], [0:16], [0:16], [0:768]} | slice | bytes 1572864 | tf_op jit(solution)/shard_map/slice | solution.py:374
  1.8 0.0 copy-start.1
  1.8 0.7 %copy-done.1 = s32[4,4,192]{2,1,0:T(4,128)S(1)} copy-done((s32[4,4,192]{2,1,0:T(4,128)S(1)}, s32[4,4,192]{2,1,0:T(4,128)}, u32[]{:S(2)}) %copy-start.1) | copy-done | bytes 12312
  2.5 0.0 copy-start.2
  2.5 0.7 %copy-done.2 = s32[4,4,192]{2,1,0:T(4,128)S(1)} copy-done((s32[4,4,192]{2,1,0:T(4,128)S(1)}, s32[4,4,192]{2,1,0:T(4,128)}, u32[]{:S(2)}) %copy-start.2) | copy-done | bytes 12312
  3.3 1.0 %fields.1.mask_ref.field_ref = f32[7,4,16,768]{3,2,1,0:T(8,128)S(1)} custom-call(s32[4,4,192]{2,1,0:T(4,128)S(1)} %copy-done.1, s32[4,4,192]{2,1,0:T(4,128)S(1)} %copy-done.2), custom_call_target="tpu_custom_call" | custom-call | tf_op jit(solution)/shard_map/fields/pallas_call | solution.py:68
  4.3 6.8 %halo0.1 = (f32[2,16,768]{2,1,0:T(8,128)S(1)}, f32[2,32,768]{2,1,0:T(8,128)S(1)}) custom-call(f32[1,16,16,768]{3,2,1,0:T(8,128)S(1)} %slice.12.v_ref, f32[7,4,16,768]{3,2,1,0:T(8,128)S(1)} %fields.1.mask_ref.field_ref), custom_call_target="tpu_custom_call" | custom-call | tf_op jit(solution)/shard_map/halo0/pallas_call | solution.py:152
  11.2 0.0 copy-start
  11.2 2.8 %copy-done = f32[8,16,16,768]{3,2,1,0:T(8,128)S(1)} copy-done((f32[8,16,16,768]{3,2,1,0:T(8,128)S(1)}, f32[8,16,16,768]{3,2,1,0:T(8,128)}, u32[]{:S(2)}) %copy-start) | copy-done | bytes 6291480
  13.9 6.0 %step.2 = (f32[8,16,16,768]{3,2,1,0:T(8,128)S(1)}, f32[6,16,768]{2,1,0:T(8,128)S(1)}) custom-call(f32[8,16,16,768]{3,2,1,0:T(8,128)S(1)} %copy-done, f32[8,16,16,768]{3,2,1,0:T(8,128)S(1)} %copy-done, f32[7,4,16,768]{3,2,1,0:T(8,128)S(1)} %fields.1.mask_ref.field_ref, f32[2,16,768]{2,1,0:T(8,128)S(1)} %get-tuple-element.10.hx_ref, ...), custom_call_target="tpu_custom_call" | custom-call | tf_op jit(solution)/shard_map/step/pallas_call | solution.py:273
  19.9 6.4 %halo1.1 = (f32[2,16,768]{2,1,0:T(8,128)S(1)}, f32[2,32,768]{2,1,0:T(8,128)S(1)}) custom-call(f32[8,16,16,768]{3,2,1,0:T(8,128)S(1)} %get-tuple-element.12.v_ref.in_ref, f32[7,4,16,768]{3,2,1,0:T(8,128)S(1)} %fields.1.mask_ref.field_ref), custom_call_target="tpu_custom_call" | custom-call | tf_op jit(solution)/shard_map/halo1/pallas_call | solution.py:152
  26.4 7.1 %step.3 = (f32[8,16,16,768]{3,2,1,0:T(8,128)}, f32[6,16,768]{2,1,0:T(8,128)S(1)}) custom-call(f32[8,16,16,768]{3,2,1,0:T(8,128)S(1)} %get-tuple-element.12.v_ref.in_ref, f32[8,16,16,768]{3,2,1,0:T(8,128)S(1)} %get-tuple-element.12.v_ref.in_ref, f32[7,4,16,768]{3,2,1,0:T(8,128)S(1)} %fields.1.mask_ref.field_ref, f32[2,16,768]{2,1,0:T(8,128)S(1)} %get-tuple-element.13.hx_ref, ...), custom_call_target="tpu_custom_call" | custom-call | tf_op jit(solution)/shard_map/step/pallas_call | solution.py:273
  33.5 0.6 %reshape.10 = f32[192,4,192]{2,1,0:T(4,128)S(1)} reshape(f32[2,6,16,768]{3,2,1,0:T(8,128)S(1)} %pad_maximum_fusion) | data formatting | bytes 1179648 | tf_op jit(solution)/shard_map/reshape | solution.py:345
  34.1 0.2 copy.7
  34.3 0.1 pad_maximum_fusion.1.refs_1_
  34.5 11.8 %blend.1 = f32[4,4,16,192]{3,2,1,0:T(8,128)S(1)} custom-call(f32[4,192,128]{2,1,0:T(8,128)S(1)} %slice.16.refs_0_, f32[4,96,128]{2,1,0:T(8,128)S(1)} %pad_maximum_fusion.1.refs_1_), custom_call_target="tpu_custom_call" | custom-call | tf_op jit(solution)/shard_map/blend/pallas_call | solution.py:354
  46.2 0.7 %copy.9 = f32[2,2,4,16,192]{4,3,2,1,0:T(8,128)} copy(f32[2,2,4,16,192]{4,3,2,1,0:T(8,128)S(1)} %bitcast.8) | data formatting | bytes 393216
  (3 shorter events, 0.1 us)
Async XLA Ops:
  1.8 0.7 %copy-start.1 = (s32[4,4,192]{2,1,0:T(4,128)S(1)}, s32[4,4,192]{2,1,0:T(4,128)}, u32[]{:S(2)}) copy-start(s32[4,4,192]{2,1,0:T(4,128)} %tissue_ref.1) | copy-start | bytes 36868
  2.5 0.7 %copy-start.2 = (s32[4,4,192]{2,1,0:T(4,128)S(1)}, s32[4,4,192]{2,1,0:T(4,128)}, u32[]{:S(2)}) copy-start(s32[4,4,192]{2,1,0:T(4,128)} %fiber_ref.1) | copy-start | bytes 36868
  11.2 2.8 %copy-start = (f32[8,16,16,768]{3,2,1,0:T(8,128)S(1)}, f32[8,16,16,768]{3,2,1,0:T(8,128)}, u32[]{:S(2)}) copy-start(f32[8,16,16,768]{3,2,1,0:T(8,128)} %v_ref.1) | copy-start | bytes 18874372
